TPU v7x, 32 devices: a whole 2x2x4 slice. The times are simulated.
32 devices in a mesh: row: 8 (over z, y), col: 4 (over x, core).
Axes of the slice: x: 2, y: 2, z: 4, core: 2. Of those that a mesh axis runs over, the one named last changes fastest.
Arguments:
- features: float32 [32, 3072], P(None, ('row', 'col')), may hold values from -6 to 6
- block: float32 [16, 3072], P(None, ('row', 'col')), may hold values from -6 to 6
Outputs:
- applied: float32 [16, 3072], P(None, ('row', 'col'))
All inputs are finite; a program needn't handle non-finite values.
Results may differ from a plain program's by a relative error of at most 0.006.
Values may be sent and summed in bfloat16 or wider, within the bound.
A program may use at most 64 MiB of HBM per device.

v0:
```python
import math

import jax
import jax.numpy as jnp
from jax import lax
from jax.sharding import PartitionSpec as P


def kernel_rows(row_feat, row_sq, col_feat, col_sq, scale, start, count):
    part = lax.dynamic_slice_in_dim(row_feat, start, count, 1)
    sq_part = lax.dynamic_slice_in_dim(row_sq, start, count, 0)
    inner = jnp.einsum("fi,fj->ij", part, col_feat, precision=lax.Precision.HIGHEST)
    dist = sq_part[:, None] + col_sq[None, :] - 2.0 * inner
    return jnp.exp(-dist / scale).astype(jnp.bfloat16)


def combine(partial_value, owned):
    whole = lax.psum(partial_value, "col")
    return lax.dynamic_slice_in_dim(whole, lax.axis_index("col") * owned, owned, 1)


def full_plan(features, block, row_feat, scale):
    owned = features.shape[1]
    col_feat = lax.all_gather(features, "row", axis=1, tiled=True)
    row_sq = jnp.sum(row_feat * row_feat, axis=0)
    col_sq = jnp.sum(col_feat * col_feat, axis=0)
    rows = row_feat.shape[1]
    step = math.gcd(512, rows)
    count_blocks = rows // step
    starts = jnp.arange(count_blocks, dtype=jnp.int32) * step
    indexes = jnp.arange(count_blocks, dtype=jnp.int32)

    def fetch(index):
        return kernel_rows(row_feat, row_sq, col_feat, col_sq, scale, starts[index], step)

    def first_pass(index):
        tile = fetch(index)
        return (jnp.sum(tile, axis=1, dtype=jnp.float32), jnp.sum(tile, axis=0, dtype=jnp.float32))

    row_parts, col_parts = lax.map(first_pass, indexes)
    q_own = combine(row_parts.reshape(1, rows), owned)
    inv_own = 1.0 / q_own
    col_total = lax.psum(jnp.sum(col_parts, axis=0)[None, :], "row")
    inv_col = 1.0 / col_total

    def second_pass(index):
        return jnp.sum(fetch(index).astype(jnp.float32) * inv_col, axis=1)

    second = combine(lax.map(second_pass, indexes).reshape(1, rows), owned)
    dens = second * inv_own
    factor = inv_own * lax.rsqrt(dens)
    weighted = (block * factor).astype(jnp.bfloat16)
    weighted_col = lax.all_gather(weighted, "row", axis=1, tiled=True)

    def third_pass(index):
        return jnp.einsum(
            "kj,ij->ki", weighted_col, fetch(index), preferred_element_type=jnp.float32
        )

    products = lax.map(third_pass, indexes)
    partial_value = jnp.moveaxis(products, 0, 1).reshape(block.shape[0], rows)
    return combine(partial_value, owned) * factor


def per_device(features, block):
    n_row = lax.axis_size("row")
    n_col = lax.axis_size("col")
    width, owned = features.shape
    frames = owned * n_row * n_col
    scale = 4.0 / (float(frames) ** (2.0 / width) - 1.0)
    row_feat = lax.all_gather(features, "col", axis=1, tiled=True)
    return full_plan(features, block, row_feat, scale)


def solution(mesh):
    placed = (P(None, ("row", "col")), P(None, ("row", "col")))
    return jax.shard_map(
        per_device, mesh=mesh, in_specs=placed, out_specs=P(None, ("row", "col")), check_vma=False
    )
```

profile of v0, /device:TPU:0, one launch (start us, length us, event | category | flops | bytes accessed | tf_op | source)
XLA Modules:
  0.0 166.0 jit_solution(17195008290931523014)
XLA Ops:
  0.0 32.5 %all-gather.1 = f32[8,96,32]{1,2,0:T(8,128)S(1)} all-gather(f32[1,96,32]{1,2,0:T(8,128)} %bitcast.84), channel_id=1, replica_groups=mesh['row'=8,'col'=4] {'row'}, dimensions={0}, use_global_device_ids=true | all-gather | bytes 110592 | tf_op jit(solution)/shard_map/all_gather | solution.py:24
  32.8 0.7 copy-done
  33.4 5.2 %all-gather = f32[4,96,32]{1,2,0:T(8,128)S(1)} all-gather(f32[1,96,32]{1,2,0:T(8,128)S(1)} %bitcast.85), channel_id=1, replica_groups=mesh['row'=8,'col'=4] {'col'}, dimensions={0}, use_global_device_ids=true | all-gather | bytes 61440 | tf_op jit(solution)/shard_map/all_gather | solution.py:71
  38.9 19.3 %while.32 = (s32[]{:T(128)}, f32[3,128]{1,0:T(4,128)S(1)}, f32[3,768]{1,0:T(4,128)S(1)}, s32[3]{0:T(128)S(1)}, s32[3]{0:T(128)S(1)}, /*index=5*/f32[384]{0:T(512...) while((s32[]{:T(128)}, f32[3,128]{1,0:T(4,128)S(1)}, ...), condition=%wide.region_5.6_spmd, body=%wide.region_2.5_spmd.sunk | while | flops 38632584 | bytes 137449 | solution.py:40
  41.6 0.7 dynamic_slice.88
  44.5 0.7 fusion.51
  48.1 0.7 dynamic_slice.88
  50.9 0.7 fusion.51
  54.5 0.7 dynamic_slice.88
  57.3 0.7 fusion.51
  58.2 21.4 %psum.29 = f32[1,768]{1,0:T(1,128)S(1)} all-reduce(f32[1,768]{1,0:T(1,128)S(1)} %broadcast_in_dim.32), channel_id=1, replica_groups=mesh['row'=8,'col'=4] {'row'}, use_global_device_ids=true, to_apply=%region_8.9 | all-reduce | flops 768 | bytes 6144 | tf_op jit(solution)/shard_map/psum | solution.py:43
  79.6 19.1 %while.33 = (s32[]{:T(128)}, f32[3,128]{1,0:T(4,128)S(1)}, s32[3]{0:T(128)S(1)}, s32[3]{0:T(128)S(1)}, f32[384]{0:T(512)S(1)}, /*index=5*/f32[768]{0:T(1024)S(1)...) while((s32[]{:T(128)}, f32[3,128]{1,0:T(4,128)S(1)}, ...), condition=%wide.region_11.12_spmd, body=%wide.region_9.11_spmd.sunk | while | flops 38633352 | bytes 132337 | solution.py:49
  82.4 0.7 dynamic_slice.92
  85.2 0.7 fusion.54
  91.6 0.7 fusion.54
  97.9 0.7 fusion.54
  98.7 5.7 %all-reduce = (f32[1,384]{1,0:T(1,128)S(1)}, f32[1,384]{1,0:T(1,128)S(1)}) all-reduce(f32[1,384]{1,0:T(1,128)S(1)} %get-tuple-element.209, f32[1,384]{1,0:T(1,128)S(1)} %get-tuple-element.210), channel_id=1, replica_groups=mesh['row'=8,'col'=4] {'col'}, use_global_device_ids=true, to_apply=%region_12.13 | all-reduce | flops 768 | bytes 6144 | tf_op jit(solution)/shard_map/psum | solution.py:18
  105.1 30.6 %all-gather.2 = bf16[8,96,16]{1,2,0:T(8,128)(2,1)S(1)} all-gather(bf16[1,96,16]{1,2,0:T(8,128)(2,1)S(1)} %fusion.26), channel_id=1, replica_groups=mesh['row'=8,'col'=4] {'row'}, dimensions={0}, use_global_device_ids=true | all-gather | bytes 27648 | tf_op jit(solution)/shard_map/all_gather | solution.py:53
  135.8 19.2 %while.34 = (s32[]{:T(128)}, f32[3,16,128]{2,1,0:T(8,128)S(1)}, s32[3]{0:T(128)S(1)}, s32[3]{0:T(128)S(1)}, f32[384]{0:T(512)S(1)}, /*index=5*/f32[768]{0:T(1024...) while((s32[]{:T(128)}, f32[3,16,128]{2,1,0:T(8,128)S(1)}, ...), condition=%wide.region_14.15_spmd, body=%wide.region_13.14_spmd.sunk | while | flops 41484296 | bytes 546533 | solution.py:60
  142.2 0.7 dynamic_slice.95
  145.0 0.7 dynamic_slice.96
  148.6 0.7 dynamic_slice.95
  155.0 10.3 %psum.31 = f32[16,384]{1,0:T(8,128)S(1)} all-reduce(f32[16,384]{1,0:T(8,128)S(1)} %copy_bitcast_fusion), channel_id=1, replica_groups=mesh['row'=8,'col'=4] {'col'}, use_global_device_ids=true, to_apply=%region_15.16 | all-reduce | flops 6144 | bytes 49152 | tf_op jit(solution)/shard_map/psum | solution.py:18
  165.3 0.7 dynamic-slice_multiply_fusion
  (67 shorter events, 12.1 us)
Async XLA Ops:
  32.7 0.7 copy-start
  104.4 0.7 copy-start.1
where the time goes:
time: 167 us; the launch traced here: 166 us
  blocking collectives  106 us (63%)
  loops' own time  37.5 us (22%)
  local copies, waits for them, and re-layouts  15 us (9%)
  matrix products  6.79 us (4%)
    all_gather x1, blocking collectives, full_plan(): col_feat = lax.all_gather(features, 'row', axis=1, tiled=True)  32.5 us
    all_gather x1, blocking collectives, full_plan(): weighted_col = lax.all_gather(weighted, 'row', axis=1, tiled=True)  30.6 us
    psum x1, blocking collectives, full_plan(): col_total = lax.psum(jnp.sum(col_parts, axis=0)[None, :], 'row')  21.4 us
    psum x2, blocking collectives, combine(): whole = lax.psum(partial_value, 'col')  16 us
    another operation x1, loops' own time, full_plan(): row_parts, col_parts = lax.map(first_pass, indexes)  12.5 us
    another operation x1, loops' own time, full_plan(): products = lax.map(third_pass, indexes)  12.5 us
    another operation x1, loops' own time, full_plan(): second = combine(lax.map(second_pass, indexes).reshape(1, rows), owned)  12.5 us
    dot_general x9, matrix products, kernel_rows(): jnp.einsum('fi,fj->ij', part, col_feat, precision=lax.Precision.HIGHEST)  6.41 us

commit v1 on v0

v1 whole, which is shorter than its diff:
```python
import math

import jax
import jax.numpy as jnp
from jax import lax
from jax.experimental import pallas as pl
from jax.experimental.pallas import tpu as pltpu
from jax.sharding import PartitionSpec as P

F32 = jnp.float32
BF16 = jnp.bfloat16


def split(value, pieces):
    out = []
    for _ in range(pieces):
        piece = value.astype(BF16).astype(F32)
        out.append(piece)
        value = value - piece
    return out


def body(
    n_a, n_b, n_y, n_col, root,
    feat_ref, block_ref, out_ref,
    pad_ref, u_ref, v_ref, blk_ref, kern_ref, csum_ref, rsum_ref, sec_ref, part_ref, got_ref, fac_ref,
    u_s, u_r, v_s, v_r, k_s, k_r, c_s, c_r, r_s, r_r, s_s, s_r, p_s, p_r,
):
    width, owned = feat_ref.shape
    row, col = lax.axis_index("row"), lax.axis_index("col")
    a = row // n_y
    b = (row % n_y) * n_col + col
    a_peers = [lax.rem(a + k, n_a) for k in range(1, n_a)]
    b_peers = [lax.rem(b + k, n_b) for k in range(1, n_b)]

    def a_dev(peer):
        return (peer * n_y + b // n_col, b % n_col)

    def b_dev(peer):
        return (a * n_y + peer // n_col, peer % n_col)

    def copy(src, dst, send, recv, dev):
        return pltpu.make_async_remote_copy(
            src_ref=src, dst_ref=dst, send_sem=send, recv_sem=recv,
            device_id=dev, device_id_type=pl.DeviceIdType.MESH,
        )

    barrier = pltpu.get_barrier_semaphore()
    for peer in a_peers:
        pl.semaphore_signal(barrier, inc=1, device_id=a_dev(peer), device_id_type=pl.DeviceIdType.MESH)
    for peer in b_peers:
        pl.semaphore_signal(barrier, inc=1, device_id=b_dev(peer), device_id_type=pl.DeviceIdType.MESH)

    pad_ref[...] = jnp.zeros_like(pad_ref)
    pad_ref[:, :owned] = feat_ref[...] * root
    hi, lo = split(pad_ref[...], 2)
    half = jnp.sum(hi * (0.5 * hi + lo), axis=0, keepdims=True)
    t = [-piece for piece in split(half, 3)]
    one = jnp.ones_like(half)
    zero = jnp.zeros((128 - 3 * width - 6, pad_ref.shape[1]), F32)
    left = jnp.concatenate([hi, lo, hi] + t + [one] * 3 + [zero], axis=0)
    right = jnp.concatenate([hi, hi, lo] + [one] * 3 + t + [zero], axis=0)
    u_ref[b] = left.T[:owned].astype(BF16)
    v_ref[a] = right.T[:owned].astype(BF16)
    blk_ref[b] = block_ref[...]

    pl.semaphore_wait(barrier, n_a + n_b - 2)

    sends = []

    def send(cp):
        cp.start()
        sends.append(cp)

    for k, peer in enumerate(a_peers):
        send(copy(v_ref.at[a], v_ref.at[a], v_s.at[k], v_r.at[a], a_dev(peer)))
    for k, peer in enumerate(b_peers):
        send(copy(u_ref.at[b], u_ref.at[b], u_s.at[k], u_r.at[b], b_dev(peer)))
    for k, peer in enumerate(b_peers):
        send(copy(block_ref, blk_ref.at[b], k_s.at[k], k_r.at[b], b_dev(peer)))

    for peer in a_peers:
        copy(v_ref.at[a], v_ref.at[peer], v_s.at[0], v_r.at[peer], a_dev(peer)).wait_recv()
    v = v_ref[...].reshape(n_a * owned, 128)

    total = jnp.zeros((8, n_a * owned), F32)
    for peer in [b] + b_peers:
        if peer is not b:
            copy(u_ref.at[b], u_ref.at[peer], u_s.at[0], u_r.at[peer], b_dev(peer)).wait_recv()
        expo = lax.dot_general(u_ref[peer], v, (((1,), (1,)), ((), ())), preferred_element_type=F32)
        tile = jnp.exp2(expo).astype(BF16)
        kern_ref[peer] = tile
        total = total + jnp.sum(tile.astype(F32).reshape(owned // 8, 8, n_a * owned), axis=0)

    csum_ref[a] = jnp.sum(total, axis=0, keepdims=True)
    for k, peer in enumerate(a_peers):
        send(copy(csum_ref.at[a], csum_ref.at[a], c_s.at[k], c_r.at[a], a_dev(peer)))

    kern = kern_ref[...].reshape(n_b * owned, n_a * owned)
    nt = (((1,), (1,)), ((), ()))
    ones = jnp.ones((16, n_a * owned), BF16)
    rsum_ref[b] = lax.dot_general(ones, kern, nt, preferred_element_type=F32)[:1]
    for k, peer in enumerate(b_peers):
        send(copy(rsum_ref.at[b], rsum_ref.at[b], r_s.at[k], r_r.at[b], b_dev(peer)))

    for peer in b_peers:
        copy(block_ref, blk_ref.at[peer], k_s.at[0], k_r.at[peer], b_dev(peer)).wait_recv()
    blocks = jnp.concatenate([blk_ref[i] for i in range(n_b)], axis=1)

    for peer in a_peers:
        copy(csum_ref.at[a], csum_ref.at[peer], c_s.at[0], c_r.at[peer], a_dev(peer)).wait_recv()
    inv_c = 1.0 / jnp.sum(csum_ref[...], axis=0)
    lhs = jnp.concatenate(split(inv_c, 3) + [jnp.zeros((13, n_a * owned), F32)], axis=0).astype(BF16)
    sec = lax.dot_general(lhs, kern, nt, preferred_element_type=F32)
    sec_ref[b] = sec[0:1] + sec[1:2] + sec[2:3]
    for k, peer in enumerate(b_peers):
        send(copy(sec_ref.at[b], sec_ref.at[b], s_s.at[k], s_r.at[b], b_dev(peer)))

    for peer in b_peers:
        copy(rsum_ref.at[b], rsum_ref.at[peer], r_s.at[0], r_r.at[peer], b_dev(peer)).wait_recv()
    inv_r = 1.0 / jnp.sum(rsum_ref[...], axis=0)
    for peer in b_peers:
        copy(sec_ref.at[b], sec_ref.at[peer], s_s.at[0], s_r.at[peer], b_dev(peer)).wait_recv()
    dens = jnp.sum(sec_ref[...], axis=0) * inv_r
    factor = inv_r * lax.rsqrt(dens)
    for i in range(n_b):
        fac_ref[i] = factor[:, i * owned:(i + 1) * owned]
    weighted = (blocks * factor).astype(BF16)
    partial = jnp.dot(weighted, kern, preferred_element_type=F32)
    for i in range(n_a):
        part_ref[i] = partial[:, i * owned:(i + 1) * owned]
    for k, peer in enumerate(a_peers):
        send(copy(part_ref.at[peer], got_ref.at[a], p_s.at[k], p_r.at[a], a_dev(peer)))
    got_ref[a] = part_ref[a]
    for peer in a_peers:
        copy(part_ref.at[a], got_ref.at[peer], p_s.at[0], p_r.at[peer], a_dev(peer)).wait_recv()
    out_ref[...] = jnp.sum(got_ref[...], axis=0) * fac_ref[b]
    for cp in sends:
        cp.wait_send()


def per_device(features, block):
    n_row = lax.axis_size("row")
    n_col = lax.axis_size("col")
    n_y = 2 if n_row % 2 == 0 else 1
    n_a, n_b = n_row // n_y, n_y * n_col
    width, owned = features.shape
    columns = block.shape[0]
    frames = owned * n_row * n_col
    scale = 4.0 / (float(frames) ** (2.0 / width) - 1.0)
    root = math.sqrt(2.0 * math.log2(math.e) / scale)
    lanes = 128 * ((owned + 127) // 128)
    dma = pltpu.SemaphoreType.DMA
    a_sem, b_sem = dma((n_a,)), dma((n_b,))

    def kernel(*refs):
        body(n_a, n_b, n_y, n_col, root, *refs)

    vmem = pl.BlockSpec(memory_space=pltpu.VMEM)
    return pl.pallas_call(
        kernel,
        out_shape=jax.ShapeDtypeStruct(block.shape, F32),
        in_specs=[vmem, vmem],
        out_specs=vmem,
        scratch_shapes=[
            pltpu.VMEM((width, lanes), F32),
            pltpu.VMEM((n_b, owned, 128), BF16),
            pltpu.VMEM((n_a, owned, 128), BF16),
            pltpu.VMEM((n_b, columns, owned), F32),
            pltpu.VMEM((n_b, owned, n_a * owned), BF16),
            pltpu.VMEM((n_a, 1, n_a * owned), F32),
            pltpu.VMEM((n_b, 1, n_b * owned), F32),
            pltpu.VMEM((n_b, 1, n_b * owned), F32),
            pltpu.VMEM((n_a, columns, owned), F32),
            pltpu.VMEM((n_a, columns, owned), F32),
            pltpu.VMEM((n_b, 1, owned), F32),
            b_sem, b_sem, a_sem, a_sem, b_sem, b_sem, a_sem, a_sem,
            b_sem, b_sem, b_sem, b_sem, a_sem, a_sem,
        ],
        compiler_params=pltpu.CompilerParams(collective_id=0, has_side_effects=True),
        name="diffusion",
    )(features, block)


def solution(mesh):
    placed = (P(None, ("row", "col")), P(None, ("row", "col")))
    return jax.shard_map(
        per_device, mesh=mesh, in_specs=placed, out_specs=P(None, ("row", "col")), check_vma=False
    )
```

time: 167 us -> 25.1 us (0.15)
  blocking collectives: 106 us -> 0 us
  loops' own time: 37.5 us -> 0 us
  Pallas kernels: 0 us -> 23.5 us
  local copies, waits for them, and re-layouts: 15 us -> 1.3 us
  matrix products: 6.79 us -> 0 us
    all_gather x3 -> x0, blocking collectives: 68.4 us -> none  [the longest x1 32.5 us: full_plan(): col_feat = lax.all_gather(features, 'row', axis=1, tiled=True)]
    another operation x3 -> x0, loops' own time: 37.5 us -> none  [the longest x1 12.5 us: full_plan(): row_parts, col_parts = lax.map(first_pass, indexes)]
    psum x3 -> x0, blocking collectives: 37.3 us -> none  [the longest x1 21.4 us: full_plan(): col_total = lax.psum(jnp.sum(col_parts, axis=0)[None, :], 'row')]
    pallas_call x0 -> x1, Pallas kernels: none -> 23.5 us  [per_device(): pl.pallas_call(kernel, out_shape=jax.ShapeDtypeStruct(block.shape, F32),...]
    dynamic_slice x27 -> x0, local copies, waits for them, and re-layouts: 12.8 us -> none  [the longest x9 6.12 us: full_plan(): row_parts, col_parts = lax.map(first_pass, indexes)]
    dot_general x12 -> x0, matrix products: 6.79 us -> none  [the longest x9 6.41 us: kernel_rows(): jnp.einsum('fi,fj->ij', part, col_feat, precision=lax.Precision.HIGHEST)]
where the time goes in v1:
time: 25.1 us; the launch traced here: 24.8 us
  Pallas kernels  23.5 us (94%)
  local copies, waits for them, and re-layouts  1.3 us (5%)
    pallas_call x1, Pallas kernels, per_device(): pl.pallas_call(kernel, out_shape=jax.ShapeDtypeStruct(block.shape, F32),...  23.5 us
    unnamed x1, local copies, waits for them, and re-layouts  1.3 us

profile of v1, /device:TPU:0, one launch (start us, length us, event | category | flops | bytes accessed | tf_op | source)
XLA Modules:
  0.0 24.8 jit_solution(3833813888004070796)
XLA Ops:
  0.0 23.5 %diffusion.1 = f32[16,96]{1,0:T(8,128)} custom-call(f32[32,96]{1,0:T(8,128)} %refs_0_.1, f32[16,96]{1,0:T(8,128)} %refs_1_.1), custom_call_target="tpu_custom_call" | custom-call | tf_op jit(solution)/shard_map/diffusion/pallas_call | solution.py:160
  23.5 1.3 %copy.4 = f32[16,96]{1,0:T(8,128)} copy(f32[16,96]{1,0:T(8,128)} %diffusion.1) | data formatting | bytes 12288

commit v2 on v1

--- a/solution.py
+++ b/solution.py
@@ -22,22 +22,22 @@
 
 def body(
     n_a, n_b, n_y, n_col, root,
-    feat_ref, block_ref, out_ref,
-    pad_ref, u_ref, v_ref, blk_ref, kern_ref, csum_ref, rsum_ref, sec_ref, part_ref, got_ref, fac_ref,
-    u_s, u_r, v_s, v_r, k_s, k_r, c_s, c_r, r_s, r_r, s_s, s_r, p_s, p_r,
+    feat_hbm, block_hbm, out_ref,
+    feat_ref, pad_ref, u_ref, v_ref, blk_ref, kern_ref, csum_ref, rsum_ref, sec_ref, part_ref, got_ref, fac_ref,
+    f_l, k_l, u_s, u_r, v_s, v_r, k_s, k_r, c_s, c_r, r_s, r_r, s_s, s_r, p_s, p_r,
 ):
     width, owned = feat_ref.shape
     row, col = lax.axis_index("row"), lax.axis_index("col")
-    a = row // n_y
-    b = (row % n_y) * n_col + col
+    a = (row % n_y) * n_col + col
+    b = row // n_y
     a_peers = [lax.rem(a + k, n_a) for k in range(1, n_a)]
     b_peers = [lax.rem(b + k, n_b) for k in range(1, n_b)]
 
     def a_dev(peer):
-        return (peer * n_y + b // n_col, b % n_col)
+        return (b * n_y + peer // n_col, peer % n_col)
 
     def b_dev(peer):
-        return (a * n_y + peer // n_col, peer % n_col)
+        return (peer * n_y + row % n_y, col)
 
     def copy(src, dst, send, recv, dev):
         return pltpu.make_async_remote_copy(
@@ -51,7 +51,12 @@
     for peer in b_peers:
         pl.semaphore_signal(barrier, inc=1, device_id=b_dev(peer), device_id_type=pl.DeviceIdType.MESH)
 
+    load = pltpu.make_async_copy(feat_hbm, feat_ref, f_l)
+    load.start()
+    load_block = pltpu.make_async_copy(block_hbm, blk_ref.at[b], k_l)
+    load_block.start()
     pad_ref[...] = jnp.zeros_like(pad_ref)
+    load.wait()
     pad_ref[:, :owned] = feat_ref[...] * root
     hi, lo = split(pad_ref[...], 2)
     half = jnp.sum(hi * (0.5 * hi + lo), axis=0, keepdims=True)
@@ -62,7 +67,6 @@
     right = jnp.concatenate([hi, hi, lo] + [one] * 3 + t + [zero], axis=0)
     u_ref[b] = left.T[:owned].astype(BF16)
     v_ref[a] = right.T[:owned].astype(BF16)
-    blk_ref[b] = block_ref[...]
 
     pl.semaphore_wait(barrier, n_a + n_b - 2)
 
@@ -77,7 +81,9 @@
     for k, peer in enumerate(b_peers):
         send(copy(u_ref.at[b], u_ref.at[b], u_s.at[k], u_r.at[b], b_dev(peer)))
     for k, peer in enumerate(b_peers):
-        send(copy(block_ref, blk_ref.at[b], k_s.at[k], k_r.at[b], b_dev(peer)))
+        if k == 0:
+            load_block.wait()
+        send(copy(blk_ref.at[b], blk_ref.at[b], k_s.at[k], k_r.at[b], b_dev(peer)))
 
     for peer in a_peers:
         copy(v_ref.at[a], v_ref.at[peer], v_s.at[0], v_r.at[peer], a_dev(peer)).wait_recv()
@@ -104,7 +110,7 @@
         send(copy(rsum_ref.at[b], rsum_ref.at[b], r_s.at[k], r_r.at[b], b_dev(peer)))
 
     for peer in b_peers:
-        copy(block_ref, blk_ref.at[peer], k_s.at[0], k_r.at[peer], b_dev(peer)).wait_recv()
+        copy(blk_ref.at[b], blk_ref.at[peer], k_s.at[0], k_r.at[peer], b_dev(peer)).wait_recv()
     blocks = jnp.concatenate([blk_ref[i] for i in range(n_b)], axis=1)
 
     for peer in a_peers:
@@ -143,7 +149,7 @@
     n_row = lax.axis_size("row")
     n_col = lax.axis_size("col")
     n_y = 2 if n_row % 2 == 0 else 1
-    n_a, n_b = n_row // n_y, n_y * n_col
+    n_a, n_b = n_y * n_col, n_row // n_y
     width, owned = features.shape
     columns = block.shape[0]
     frames = owned * n_row * n_col
@@ -156,13 +162,14 @@
     def kernel(*refs):
         body(n_a, n_b, n_y, n_col, root, *refs)
 
-    vmem = pl.BlockSpec(memory_space=pltpu.VMEM)
+    hbm = pl.BlockSpec(memory_space=pltpu.HBM)
     return pl.pallas_call(
         kernel,
-        out_shape=jax.ShapeDtypeStruct(block.shape, F32),
-        in_specs=[vmem, vmem],
-        out_specs=vmem,
+        out_shape=pltpu.VMEM(block.shape, F32),
+        in_specs=[hbm, hbm],
+        out_specs=pl.BlockSpec(memory_space=pltpu.VMEM),
         scratch_shapes=[
+            pltpu.VMEM(features.shape, F32),
             pltpu.VMEM((width, lanes), F32),
             pltpu.VMEM((n_b, owned, 128), BF16),
             pltpu.VMEM((n_a, owned, 128), BF16),
@@ -174,7 +181,7 @@
             pltpu.VMEM((n_a, columns, owned), F32),
             pltpu.VMEM((n_a, columns, owned), F32),
             pltpu.VMEM((n_b, 1, owned), F32),
-            b_sem, b_sem, a_sem, a_sem, b_sem, b_sem, a_sem, a_sem,
+            dma, dma, b_sem, b_sem, a_sem, a_sem, b_sem, b_sem, a_sem, a_sem,
             b_sem, b_sem, b_sem, b_sem, a_sem, a_sem,
         ],
         compiler_params=pltpu.CompilerParams(collective_id=0, has_side_effects=True),

time: 25.1 us -> 22.2 us (0.88)
  Pallas kernels: 23.5 us -> 21.3 us
  local copies, waits for them, and re-layouts: 1.3 us -> 0.6 us
    pallas_call x1, Pallas kernels: 23.5 us -> 21.3 us  [per_device(): pl.pallas_call(kernel, out_shape=pltpu.VMEM(block.shape, F32), in_specs=[...]
    unnamed x1, local copies, waits for them, and re-layouts: 1.3 us -> 0.6 us
where the time goes in v2:
time: 22.2 us; the launch traced here: 21.9 us
  Pallas kernels  21.3 us (96%)
  local copies, waits for them, and re-layouts  0.6 us (3%)
    pallas_call x1, Pallas kernels, per_device(): pl.pallas_call(kernel, out_shape=pltpu.VMEM(block.shape, F32), in_specs=[...  21.3 us
    unnamed x1, local copies, waits for them, and re-layouts  0.6 us

profile of v2, /device:TPU:0, one launch (start us, length us, event | category | flops | bytes accessed | tf_op | source)
XLA Modules:
  0.0 21.9 jit_solution(11352650184160277773)
XLA Ops:
  0.0 21.3 %diffusion.1 = f32[16,96]{1,0:T(8,128)S(1)} custom-call(f32[32,96]{1,0:T(8,128)} %refs_0_.1, f32[16,96]{1,0:T(8,128)} %refs_1_.1), custom_call_target="tpu_custom_call" | custom-call | tf_op jit(solution)/shard_map/diffusion/pallas_call | solution.py:166
  21.3 0.6 %copy.4 = f32[16,96]{1,0:T(8,128)} copy(f32[16,96]{1,0:T(8,128)S(1)} %diffusion.1) | data formatting | bytes 12288

commit v3 on v2

--- a/solution.py
+++ b/solution.py
@@ -80,10 +80,6 @@
         send(copy(v_ref.at[a], v_ref.at[a], v_s.at[k], v_r.at[a], a_dev(peer)))
     for k, peer in enumerate(b_peers):
         send(copy(u_ref.at[b], u_ref.at[b], u_s.at[k], u_r.at[b], b_dev(peer)))
-    for k, peer in enumerate(b_peers):
-        if k == 0:
-            load_block.wait()
-        send(copy(blk_ref.at[b], blk_ref.at[b], k_s.at[k], k_r.at[b], b_dev(peer)))
 
     for peer in a_peers:
         copy(v_ref.at[a], v_ref.at[peer], v_s.at[0], v_r.at[peer], a_dev(peer)).wait_recv()
@@ -102,16 +98,16 @@
     for k, peer in enumerate(a_peers):
         send(copy(csum_ref.at[a], csum_ref.at[a], c_s.at[k], c_r.at[a], a_dev(peer)))
 
+    load_block.wait()
+    for k, peer in enumerate(b_peers):
+        send(copy(blk_ref.at[b], blk_ref.at[b], k_s.at[k], k_r.at[b], b_dev(peer)))
+
     kern = kern_ref[...].reshape(n_b * owned, n_a * owned)
     nt = (((1,), (1,)), ((), ()))
     ones = jnp.ones((16, n_a * owned), BF16)
     rsum_ref[b] = lax.dot_general(ones, kern, nt, preferred_element_type=F32)[:1]
     for k, peer in enumerate(b_peers):
         send(copy(rsum_ref.at[b], rsum_ref.at[b], r_s.at[k], r_r.at[b], b_dev(peer)))
-
-    for peer in b_peers:
-        copy(blk_ref.at[b], blk_ref.at[peer], k_s.at[0], k_r.at[peer], b_dev(peer)).wait_recv()
-    blocks = jnp.concatenate([blk_ref[i] for i in range(n_b)], axis=1)
 
     for peer in a_peers:
         copy(csum_ref.at[a], csum_ref.at[peer], c_s.at[0], c_r.at[peer], a_dev(peer)).wait_recv()
@@ -124,6 +120,10 @@
 
     for peer in b_peers:
         copy(rsum_ref.at[b], rsum_ref.at[peer], r_s.at[0], r_r.at[peer], b_dev(peer)).wait_recv()
+    for peer in b_peers:
+        copy(blk_ref.at[b], blk_ref.at[peer], k_s.at[0], k_r.at[peer], b_dev(peer)).wait_recv()
+    blocks = jnp.concatenate([blk_ref[i] for i in range(n_b)], axis=1)
+
     inv_r = 1.0 / jnp.sum(rsum_ref[...], axis=0)
     for peer in b_peers:
         copy(sec_ref.at[b], sec_ref.at[peer], s_s.at[0], s_r.at[peer], b_dev(peer)).wait_recv()

time: 22.2 us -> 22.2 us (level)
  no operation moved by 1% of the time
where the time goes in v3:
time: 22.2 us; the launch traced here: 21.9 us
  Pallas kernels  21.3 us (96%)
  local copies, waits for them, and re-layouts  0.6 us (3%)
    pallas_call x1, Pallas kernels, per_device(): pl.pallas_call(kernel, out_shape=pltpu.VMEM(block.shape, F32), in_specs=[...  21.3 us
    unnamed x1, local copies, waits for them, and re-layouts  0.6 us

profile of v3, /device:TPU:0, one launch (start us, length us, event | category | flops | bytes accessed | tf_op | source)
XLA Modules:
  0.0 21.9 jit_solution(12126487000019768823)
XLA Ops:
  0.0 21.3 %diffusion.1 = f32[16,96]{1,0:T(8,128)S(1)} custom-call(f32[32,96]{1,0:T(8,128)} %refs_0_.1, f32[16,96]{1,0:T(8,128)} %refs_1_.1), custom_call_target="tpu_custom_call" | custom-call | tf_op jit(solution)/shard_map/diffusion/pallas_call | solution.py:166
  21.3 0.6 %copy.4 = f32[16,96]{1,0:T(8,128)} copy(f32[16,96]{1,0:T(8,128)S(1)} %diffusion.1) | data formatting | bytes 12288

commit v4 on v3

--- a/solution.py
+++ b/solution.py
@@ -20,10 +20,47 @@
     return out
 
 
+def packable(width, owned):
+    spare = 128 - owned
+    if spare <= 0 or owned % spare:
+        return False
+    rest = width * spare // 128
+    return rest % 8 == 0 and rest * (owned // spare) == width - rest
+
+
+def pack(value):
+    width, owned = value.shape
+    if not packable(width, owned):
+        return value
+    spare = 128 - owned
+    kept = width - width * spare // 128
+    rest = [value[kept:, i * spare:(i + 1) * spare] for i in range(owned // spare)]
+    return jnp.concatenate([value[:kept], jnp.concatenate(rest, axis=0)], axis=1)
+
+
+def unpack(value, width, owned):
+    if not packable(width, owned):
+        return value
+    rest = width - value.shape[0]
+    parts = [value[i * rest:(i + 1) * rest, owned:] for i in range(value.shape[0] // rest)]
+    return jnp.concatenate([value[:, :owned], jnp.concatenate(parts, axis=1)], axis=0)
+
+
+def operand(value, is_left):
+    width = value.shape[0]
+    hi, lo = split(value, 2)
+    half = jnp.sum(hi * (0.5 * hi + lo), axis=0, keepdims=True)
+    t = [-piece for piece in split(half, 3)]
+    one = [jnp.ones_like(half)] * 3
+    zero = [jnp.zeros((128 - 3 * width - 6, value.shape[1]), F32)]
+    parts = [hi, lo, hi] + t + one + zero if is_left else [hi, hi, lo] + one + t + zero
+    return jnp.concatenate(parts, axis=0).T.astype(BF16)
+
+
 def body(
     n_a, n_b, n_y, n_col, root,
     feat_hbm, block_hbm, out_ref,
-    feat_ref, pad_ref, u_ref, v_ref, blk_ref, kern_ref, csum_ref, rsum_ref, sec_ref, part_ref, got_ref, fac_ref,
+    feat_ref, x_a, x_b, u_ref, v_ref, blk_ref, kern_ref, csum_ref, rsum_ref, sec_ref, part_ref, got_ref, fac_ref,
     f_l, k_l, u_s, u_r, v_s, v_r, k_s, k_r, c_s, c_r, r_s, r_r, s_s, s_r, p_s, p_r,
 ):
     width, owned = feat_ref.shape
@@ -55,18 +92,11 @@
     load.start()
     load_block = pltpu.make_async_copy(block_hbm, blk_ref.at[b], k_l)
     load_block.start()
-    pad_ref[...] = jnp.zeros_like(pad_ref)
     load.wait()
-    pad_ref[:, :owned] = feat_ref[...] * root
-    hi, lo = split(pad_ref[...], 2)
-    half = jnp.sum(hi * (0.5 * hi + lo), axis=0, keepdims=True)
-    t = [-piece for piece in split(half, 3)]
-    one = jnp.ones_like(half)
-    zero = jnp.zeros((128 - 3 * width - 6, pad_ref.shape[1]), F32)
-    left = jnp.concatenate([hi, lo, hi] + t + [one] * 3 + [zero], axis=0)
-    right = jnp.concatenate([hi, hi, lo] + [one] * 3 + t + [zero], axis=0)
-    u_ref[b] = left.T[:owned].astype(BF16)
-    v_ref[a] = right.T[:owned].astype(BF16)
+    own = feat_ref[...] * root
+    packed = pack(own)
+    x_a[a] = packed
+    x_b[b] = packed
 
     pl.semaphore_wait(barrier, n_a + n_b - 2)
 
@@ -77,18 +107,25 @@
         sends.append(cp)
 
     for k, peer in enumerate(a_peers):
-        send(copy(v_ref.at[a], v_ref.at[a], v_s.at[k], v_r.at[a], a_dev(peer)))
-    for k, peer in enumerate(b_peers):
-        send(copy(u_ref.at[b], u_ref.at[b], u_s.at[k], u_r.at[b], b_dev(peer)))
-
-    for peer in a_peers:
-        copy(v_ref.at[a], v_ref.at[peer], v_s.at[0], v_r.at[peer], a_dev(peer)).wait_recv()
+        send(copy(x_a.at[a], x_a.at[a], v_s.at[k], v_r.at[a], a_dev(peer)))
+    for k, peer in enumerate(b_peers):
+        send(copy(x_b.at[b], x_b.at[b], u_s.at[k], u_r.at[b], b_dev(peer)))
+
+    v_ref[a] = operand(own, False)
+    u_ref[b] = operand(own, True)
+    for peer in a_peers:
+        copy(x_a.at[a], x_a.at[peer], v_s.at[0], v_r.at[peer], a_dev(peer)).wait_recv()
+    for peer in a_peers:
+        v_ref[peer] = operand(unpack(x_a[peer], width, owned), False)
     v = v_ref[...].reshape(n_a * owned, 128)
 
     total = jnp.zeros((8, n_a * owned), F32)
-    for peer in [b] + b_peers:
-        if peer is not b:
-            copy(u_ref.at[b], u_ref.at[peer], u_s.at[0], u_r.at[peer], b_dev(peer)).wait_recv()
+    for n, peer in enumerate([b] + b_peers):
+        if n == 1:
+            for other in b_peers:
+                copy(x_b.at[b], x_b.at[other], u_s.at[0], u_r.at[other], b_dev(other)).wait_recv()
+            for other in b_peers:
+                u_ref[other] = operand(unpack(x_b[other], width, owned), True)
         expo = lax.dot_general(u_ref[peer], v, (((1,), (1,)), ((), ())), preferred_element_type=F32)
         tile = jnp.exp2(expo).astype(BF16)
         kern_ref[peer] = tile
@@ -155,7 +192,7 @@
     frames = owned * n_row * n_col
     scale = 4.0 / (float(frames) ** (2.0 / width) - 1.0)
     root = math.sqrt(2.0 * math.log2(math.e) / scale)
-    lanes = 128 * ((owned + 127) // 128)
+    wire = jax.eval_shape(pack, features).shape
     dma = pltpu.SemaphoreType.DMA
     a_sem, b_sem = dma((n_a,)), dma((n_b,))
 
@@ -170,7 +207,8 @@
         out_specs=pl.BlockSpec(memory_space=pltpu.VMEM),
         scratch_shapes=[
             pltpu.VMEM(features.shape, F32),
-            pltpu.VMEM((width, lanes), F32),
+            pltpu.VMEM((n_a,) + wire, F32),
+            pltpu.VMEM((n_b,) + wire, F32),
             pltpu.VMEM((n_b, owned, 128), BF16),
             pltpu.VMEM((n_a, owned, 128), BF16),
             pltpu.VMEM((n_b, columns, owned), F32),

time: 22.2 us -> 21.6 us (0.973)
  Pallas kernels: 21.3 us -> 20.8 us
    pallas_call x1, Pallas kernels: 21.3 us -> 20.8 us  [per_device(): pl.pallas_call(kernel, out_shape=pltpu.VMEM(block.shape, F32), in_specs=[...]
where the time goes in v4:
time: 21.6 us; the launch traced here: 21.4 us
  Pallas kernels  20.8 us (96%)
  local copies, waits for them, and re-layouts  0.6 us (3%)
    pallas_call x1, Pallas kernels, per_device(): pl.pallas_call(kernel, out_shape=pltpu.VMEM(block.shape, F32), in_specs=[...  20.8 us
    unnamed x1, local copies, waits for them, and re-layouts  0.6 us

profile of v4, /device:TPU:0, one launch (start us, length us, event | category | flops | bytes accessed | tf_op | source)
XLA Modules:
  0.0 21.4 jit_solution(2713775275211871904)
XLA Ops:
  0.0 20.8 %diffusion.1 = f32[16,96]{1,0:T(8,128)S(1)} custom-call(f32[32,96]{1,0:T(8,128)} %refs_0_.1, f32[16,96]{1,0:T(8,128)} %refs_1_.1), custom_call_target="tpu_custom_call" | custom-call | tf_op jit(solution)/shard_map/diffusion/pallas_call | solution.py:203
  20.8 0.6 %copy.4 = f32[16,96]{1,0:T(8,128)} copy(f32[16,96]{1,0:T(8,128)S(1)} %diffusion.1) | data formatting | bytes 12288

commit v5 on v4

--- a/solution.py
+++ b/solution.py
@@ -106,10 +106,10 @@
         cp.start()
         sends.append(cp)
 
+    for k, peer in enumerate(b_peers):
+        send(copy(x_b.at[b], x_b.at[b], u_s.at[k], u_r.at[b], b_dev(peer)))
     for k, peer in enumerate(a_peers):
         send(copy(x_a.at[a], x_a.at[a], v_s.at[k], v_r.at[a], a_dev(peer)))
-    for k, peer in enumerate(b_peers):
-        send(copy(x_b.at[b], x_b.at[b], u_s.at[k], u_r.at[b], b_dev(peer)))
 
     v_ref[a] = operand(own, False)
     u_ref[b] = operand(own, True)

time: 21.6 us -> 21.6 us (level)
  no operation moved by 1% of the time
where the time goes in v5:
time: 21.6 us; the launch traced here: 21.4 us
  Pallas kernels  20.8 us (96%)
  local copies, waits for them, and re-layouts  0.6 us (3%)
    pallas_call x1, Pallas kernels, per_device(): pl.pallas_call(kernel, out_shape=pltpu.VMEM(block.shape, F32), in_specs=[...  20.8 us
    unnamed x1, local copies, waits for them, and re-layouts  0.6 us

profile of v5, /device:TPU:0, one launch (start us, length us, event | category | flops | bytes accessed | tf_op | source)
XLA Modules:
  0.0 21.4 jit_solution(2211411642257869717)
XLA Ops:
  0.0 20.8 %diffusion.1 = f32[16,96]{1,0:T(8,128)S(1)} custom-call(f32[32,96]{1,0:T(8,128)} %refs_0_.1, f32[16,96]{1,0:T(8,128)} %refs_1_.1), custom_call_target="tpu_custom_call" | custom-call | tf_op jit(solution)/shard_map/diffusion/pallas_call | solution.py:203
  20.8 0.6 %copy.4 = f32[16,96]{1,0:T(8,128)} copy(f32[16,96]{1,0:T(8,128)S(1)} %diffusion.1) | data formatting | bytes 12288
